TPU v7x, 32 devices: a whole 2x2x4 slice. The times are simulated.
32 devices in a mesh: rep: 2 (over x), shard: 16 (over z, y, core).
Axes of the slice: x: 2, y: 2, z: 4, core: 2. Of those that a mesh axis runs over, the one named last changes fastest.
Arguments:
- tokens: bfloat16 [4096, 2048], P(('rep', 'shard')), may hold values from -6 to 6
- segment_ids: int32 [4096], P(('rep', 'shard')), may hold values from -1 to 31, as said below
- cotangent: bfloat16 [4096, 2048], P(('rep', 'shard')), may hold values from -6 to 6
- w_qkv: bfloat16 [2048, 6144], P('shard'), may hold values from -0.125 to 0.125
- w_out: bfloat16 [2048, 2048], P('shard'), may hold values from -0.125 to 0.125
- w_gate_up: bfloat16 [2048, 16384], P('shard'), may hold values from -0.125 to 0.125
- w_down: bfloat16 [8192, 2048], P('shard'), may hold values from -0.0625 to 0.0625
- q_gain: bfloat16 [2048], P('shard'), may hold values from 0.5 to 1.5
- k_gain: bfloat16 [2048], P('shard'), may hold values from 0.5 to 1.5
- attn_gain: bfloat16 [2048], P('shard'), may hold values from 0.5 to 1.5
- mlp_gain: bfloat16 [2048], P('shard'), may hold values from 0.5 to 1.5
Outputs:
- output: bfloat16 [4096, 2048], P(('rep', 'shard'))
- grad_tokens: float32 [4096, 2048], P(('rep', 'shard'))
- grad_qkv: float32 [2048, 6144], P('shard')
- grad_out: float32 [2048, 2048], P('shard')
- grad_gate_up: float32 [2048, 16384], P('shard')
- grad_down: float32 [8192, 2048], P('shard')
- grad_q_gain: float32 [2048], P('shard')
- grad_k_gain: float32 [2048], P('shard')
- grad_attn_gain: float32 [2048], P('shard')
- grad_mlp_gain: float32 [2048], P('shard')
Inputs may be any that keep to these rules, and one draw needn't show every extreme that they name: `segment_ids`: within each block of 128 slots, live slots come first in runs of equal ids numbered upwards from 0 (one packed sequence each), each run starting at a slot whose index within the block is a multiple of 4, then padding slots with id -1; at least one block has no padding and starts a run at every multiple of 4.
All inputs are finite; a program needn't handle non-finite values.
Results may differ from a plain program's by a relative error of at most 0.02.
Values may be sent and summed in bfloat16 or wider, within the bound.
A program may use at most 384 MiB of HBM per device.

v0:
```python
import jax
import jax.numpy as jnp
from jax import lax
from jax.sharding import PartitionSpec as P

H = 16
EPSILON = 1e-06
THETA = 500000.0
BF = jnp.bfloat16
F32 = jnp.float32


def positions(seg):
    slots = lax.broadcasted_iota(jnp.int32, seg.shape, 1)
    starts = jnp.concatenate(
        [jnp.ones((seg.shape[0], 1), jnp.bool_), seg[:, 1:] != seg[:, :-1]], axis=1
    )
    first = lax.cummax(jnp.where(starts, slots, 0), axis=1)
    return slots - first


def rope_tables(seg, head_width):
    half_width = head_width // 2
    spots = positions(seg).astype(F32).reshape(-1)
    inverse = THETA ** (-(2.0 * jnp.arange(half_width, dtype=F32)) / head_width)
    angle = spots[:, None] * inverse[None, :]
    return (jnp.cos(angle), jnp.sin(angle))


def rotate(matrix, cosine, sine):
    half = matrix.shape[-1] // 2
    a, b = (matrix[..., :half], matrix[..., half:])
    return jnp.concatenate([a * cosine - b * sine, b * cosine + a * sine], axis=-1)


def mm(left, right):
    return jnp.dot(left, right, preferred_element_type=F32)


def mm_nt(left, right):
    return lax.dot_general(left, right, (((1,), (1,)), ((), ())), preferred_element_type=F32)


def mm_tn(left, right):
    return lax.dot_general(left, right, (((0,), (0,)), ((), ())), preferred_element_type=F32)


def norm_scale(vector):
    return lax.rsqrt(jnp.mean(vector * vector, axis=-1, keepdims=True) + EPSILON)


def norm_back(upstream, normed, rscale, gain):
    scaled = upstream * gain
    inner = jnp.mean(scaled * normed, axis=-1, keepdims=True)
    return (rscale * (scaled - normed * inner), jnp.sum(upstream * normed, axis=0))


def gather(piece):
    return lax.all_gather(piece, "shard", axis=0, tiled=True)


def scatter(partial):
    return lax.psum_scatter(partial.astype(BF), "shard", scatter_dimension=0, tiled=True).astype(
        F32
    )


def make(n_rep, n_shard):

    def rep_scatter(x):
        if n_rep == 2:
            me = lax.axis_index("rep")
            mine = lax.dynamic_index_in_dim(x, me, 0, keepdims=False)
            other = lax.dynamic_index_in_dim(x, 1 - me, 0, keepdims=False)
            got = lax.ppermute(other.astype(BF), "rep", [(0, 1), (1, 0)])
            return (mine + got.astype(F32)).astype(BF)
        return lax.psum_scatter(x.astype(BF), "rep", scatter_dimension=0, tiled=False)

    def rep_gather(x):
        if n_rep == 2:
            me = lax.axis_index("rep")
            got = lax.ppermute(x, "rep", [(0, 1), (1, 0)])
            first = jnp.where(me == 0, x, got)
            second = jnp.where(me == 0, got, x)
            return jnp.stack([first, second])
        return lax.all_gather(x, "rep", axis=0, tiled=False)

    def rep_sum(x):
        rows = x.shape[0]
        part = rep_scatter(x.reshape(n_rep, rows // n_rep, x.shape[1]))
        return rep_gather(part).reshape(x.shape).astype(F32)

    def grad_back(x, groups):
        rows, cols = x.shape
        own = rows // n_shard
        width = cols // groups
        split = x.reshape(n_shard, n_rep, own // n_rep, cols).transpose(1, 0, 2, 3)
        part = rep_scatter(split)
        part = lax.all_to_all(part, "shard", split_axis=0, concat_axis=0, tiled=True)
        whole = rep_gather(part)
        whole = whole.reshape(n_rep, n_shard, own // n_rep, groups, width)
        return whole.transpose(0, 2, 3, 1, 4).reshape(own, groups * n_shard * width).astype(F32)

    def columns(w, groups):
        rows, cols = w.shape
        w = w.reshape(rows, groups, n_shard, cols // (groups * n_shard))
        w = lax.all_to_all(w, "shard", split_axis=2, concat_axis=0, tiled=True)
        return w.reshape(rows * n_shard, cols // n_shard)

    def shards(
        tokens,
        segment_ids,
        cotangent,
        w_qkv,
        w_out,
        w_gate_up,
        w_down,
        q_gain,
        k_gain,
        attn_gain,
        mlp_gain,
    ):
        count, width = tokens.shape
        heads = H // n_shard
        hw = width // H
        own = width // n_shard
        ff = w_down.shape[0]
        total = count * n_shard
        small = gather(jnp.stack([segment_ids.astype(BF), attn_gain, mlp_gain])[None])
        tokens_g = gather(tokens)
        wq = columns(w_qkv, 3)
        wg = columns(w_gate_up, 2)
        seg = small[:, 0].astype(jnp.int32)
        gain_attn = small[:, 1].reshape(-1).astype(F32)
        gain_mlp = small[:, 2].reshape(-1).astype(F32)
        gain_query = q_gain.astype(F32)
        gain_keys = k_gain.astype(F32)
        cosine, sine = rope_tables(seg, hw)
        cos3 = cosine[:, None, :]
        sin3 = sine[:, None, :]
        qkv = mm(tokens_g, wq)
        query, keys, values_b = (qkv[:, :own], qkv[:, own : 2 * own], qkv[:, 2 * own :].astype(BF))
        squares = jnp.stack([jnp.sum(query * query, axis=-1), jnp.sum(keys * keys, axis=-1)])
        squares = lax.psum(squares, "shard")
        scales = lax.rsqrt(squares / width + EPSILON)
        query_scale, keys_scale = (scales[0][:, None], scales[1][:, None])
        query_hat, keys_hat = (query * query_scale, keys * keys_scale)

        def rot(x, sign):
            return rotate(x.reshape(total, heads, hw), cos3, sign * sin3).reshape(total, own)

        query_rot = rot(query_hat * gain_query, 1.0).astype(BF)
        keys_rot = rot(keys_hat * gain_keys, 1.0).astype(BF)
        slots = jnp.arange(count)
        ok = (seg[:, :, None] == seg[:, None, :]) & (slots[None, :] <= slots[:, None])[None]
        ok = ok[:, None]

        def blocks(x):
            return x.reshape(n_shard, count, heads, hw)

        root = hw ** (-0.5)
        qb, kb, vb = (blocks(query_rot), blocks(keys_rot), blocks(values_b))
        scores = jnp.einsum("bthd,bshd->bhts", qb, kb, preferred_element_type=F32) * root
        scores = jnp.where(ok, scores, -1e30)
        top = jnp.max(scores, axis=-1, keepdims=True)
        lse = top + jnp.log(jnp.sum(jnp.exp(scores - top), axis=-1, keepdims=True))
        probs = jnp.exp(scores - lse)
        probs_b = probs.astype(BF)
        context = jnp.einsum("bhts,bshd->bthd", probs_b, vb, preferred_element_type=F32)
        context_b = context.astype(BF).reshape(total, own)
        attn_raw = scatter(mm(context_b, w_out))
        attn_scale = norm_scale(attn_raw)
        attn_hat = attn_raw * attn_scale
        resid = tokens.astype(F32) + attn_hat * gain_attn
        resid_g = gather(resid.astype(BF))
        gate_up = mm(resid_g, wg)
        gate, up = (gate_up[:, :ff], gate_up[:, ff:])
        sigma = jax.nn.sigmoid(gate)
        activated = gate * sigma
        mixed_b = (activated * up).astype(BF)
        down_raw = scatter(mm(mixed_b, w_down))
        down_scale = norm_scale(down_raw)
        down_hat = down_raw * down_scale
        output = (resid + down_hat * gain_mlp).astype(BF)
        valid = (segment_ids >= 0).astype(F32)[:, None]
        d_out = cotangent.astype(F32) * valid
        d_down, grad_mlp = norm_back(d_out, down_hat, down_scale, gain_mlp)
        d_down_g = gather(d_down.astype(BF))
        d_mixed = mm_nt(d_down_g, w_down)
        d_gate = d_mixed * up * sigma * (1.0 + gate * (1.0 - sigma))
        d_up = d_mixed * activated
        d_gu_b = jnp.concatenate([d_gate, d_up], axis=1).astype(BF)
        d_resid = d_out + scatter(mm_nt(d_gu_b, wg))
        grad_down = rep_sum(mm_tn(mixed_b, d_down_g))
        grad_gu = grad_back(mm_tn(resid_g, d_gu_b), 2)
        d_attn, grad_attn = norm_back(d_resid, attn_hat, attn_scale, gain_attn)
        d_attn_g = gather(d_attn.astype(BF))
        d_context_b = mm_nt(d_attn_g, w_out).astype(BF)
        grad_out = rep_sum(mm_tn(context_b, d_attn_g))
        db = blocks(d_context_b)
        d_values = jnp.einsum("bhts,bthd->bshd", probs_b, db, preferred_element_type=F32)
        d_probs = jnp.einsum("bthd,bshd->bhts", db, vb, preferred_element_type=F32)
        delta = jnp.sum(db.astype(F32) * context, axis=-1).transpose(0, 2, 1)[..., None]
        d_scores_b = (probs * (d_probs - delta) * root).astype(BF)
        d_query_rot = jnp.einsum("bhts,bshd->bthd", d_scores_b, kb, preferred_element_type=F32)
        d_keys_rot = jnp.einsum("bhts,bthd->bshd", d_scores_b, qb, preferred_element_type=F32)
        d_query_norm = rot(d_query_rot, -1.0)
        d_keys_norm = rot(d_keys_rot, -1.0)
        grad_query = jnp.sum(d_query_norm * query_hat, axis=0)
        grad_keys = jnp.sum(d_keys_norm * keys_hat, axis=0)
        query_up = d_query_norm * gain_query
        keys_up = d_keys_norm * gain_keys
        inner = jnp.stack(
            [jnp.sum(query_up * query_hat, axis=-1), jnp.sum(keys_up * keys_hat, axis=-1)]
        )
        inner = lax.psum(inner, "shard") / width
        d_query = query_scale * (query_up - query_hat * inner[0][:, None])
        d_keys = keys_scale * (keys_up - keys_hat * inner[1][:, None])
        d_qkv_b = jnp.concatenate([d_query, d_keys, d_values.reshape(total, own)], axis=1).astype(
            BF
        )
        grad_tokens = d_resid + scatter(mm_nt(d_qkv_b, wq))
        grad_qkv = grad_back(mm_tn(tokens_g, d_qkv_b), 3)
        gains_local = lax.psum_scatter(
            jnp.stack([grad_attn, grad_mlp]), "shard", scatter_dimension=1, tiled=True
        )
        gains = lax.psum(jnp.concatenate([gains_local, jnp.stack([grad_query, grad_keys])]), "rep")
        return (
            output,
            grad_tokens,
            grad_qkv,
            grad_out,
            grad_gu,
            grad_down,
            gains[2],
            gains[3],
            gains[0],
            gains[1],
        )

    return shards


def solution(mesh):
    rows = P(("rep", "shard"), None)
    return jax.shard_map(
        make(mesh.shape["rep"], mesh.shape["shard"]),
        mesh=mesh,
        in_specs=(rows, P(("rep", "shard")), rows) + (P("shard", None),) * 4 + (P("shard"),) * 4,
        out_specs=(rows, rows) + (P("shard", None),) * 4 + (P("shard"),) * 4,
        check_vma=False,
    )
```

profile of v0, /device:TPU:0, one launch (start us, length us, event | category | flops | bytes accessed | tf_op | source)
XLA Modules:
  0.0 1212.3 jit_solution(16660373175642401086)
XLA Ops:
  13.3 7.5 all-to-all-start
  20.9 58.7 %all-gather.1 = bf16[16,3,128]{2,1,0:T(4,128)(2,1)S(1)} all-gather(bf16[1,3,128]{2,1,0:T(4,128)(2,1)S(1)} %maximum_bitcast_fusion.2), channel_id=2, replica_groups=mesh['rep'=2,'shard'=16] {'shard'}, dimensions={0}, use_global_device_ids=true | all-gather | bytes 13056 | tf_op jit(solution)/shard_map/all_gather | solution.py:59
  80.1 3.6 copy.115
  83.7 29.8 %all-gather.7.cloned.1.call-done = bf16[2048,2048]{1,0:T(8,128)(2,1)} async-done(((bf16[128,2048]{1,0:T(8,128)(2,1)}), bf16[2048,2048]{1,0:T(8,128)(2,1)}) %all-gather.7.cloned.1.call-update) | async-done | bytes 8388624 | tf_op jit(solution)/shard_map/all_gather | solution.py:59
  113.5 6.4 fusion.13
  122.4 58.7 %psum.21 = f32[2,2048]{1,0:T(2,128)S(1)} all-reduce(f32[2,2048]{1,0:T(2,128)S(1)} %pad_maximum_fusion.10), channel_id=1, replica_groups=mesh['rep'=2,'shard'=16] {'shard'}, use_global_device_ids=true, to_apply=%region_2.3 | all-reduce | flops 4096 | bytes 32768 | tf_op jit(solution)/shard_map/psum | solution.py:144
  195.0 6.8 convolution_convert_fusion.3
  201.9 100.9 %reduce-scatter.8.cloned.1.call-done = bf16[128,2048]{1,0:T(8,128)(2,1)} async-done(((bf16[2048,2048]{1,0:T(8,128)(2,1)}), bf16[128,2048]{1,0:T(8,128)(2,1)}) %reduce-scatter.8.cloned.1.call-update) | async-done | bytes 524304 | tf_op jit(solution)/shard_map/reduce_scatter | solution.py:63
  306.4 6.4 copy.120
  312.7 2.7 copy.121
  315.5 142.0 %all_to_all.40 = bf16[128,2,16,512]{0,3,1,2:T(8,128)(2,1)S(1)} all-to-all(bf16[128,2,16,512]{0,3,1,2:T(8,128)(2,1)S(1)} %copy.121), channel_id=1, replica_groups=mesh['rep'=2,'shard'=16] {'shard'}, dimensions={2} | all-to-all | bytes 8388608 | tf_op jit(solution)/shard_map/all_to_all | solution.py:107
  457.5 4.7 copy.122
  462.2 12.6 %fusion.3 = f32[2048,1024]{0,1:T(8,128)S(1)} fusion(bf16[2048,2048]{1,0:T(8,128)(2,1)} %all-gather.9.cloned.1.call-done, bf16[128,8,16,128]{3,2,1,0:T(8,128)(2,1)} %bitcast.203), kind=kOutput, calls=%fused_computation.8 | convolution fusion | flops 8589934592 | bytes 20971520 | tf_op jit(solution)/shard_map/dot_general | solution.py:37
  479.4 6.8 convolution_convert_fusion.2
  486.3 103.5 %reduce-scatter.10.cloned.1.call-done = bf16[128,2048]{1,0:T(8,128)(2,1)} async-done(((bf16[2048,2048]{1,0:T(8,128)(2,1)}), bf16[128,2048]{1,0:T(8,128)(2,1)}) %reduce-scatter.10.cloned.1.call-update) | async-done | bytes 524304 | tf_op jit(solution)/shard_map/reduce_scatter | solution.py:63
  595.4 73.9 %all-gather.11.cloned.1.call-done = bf16[2048,2048]{1,0:T(8,128)(2,1)} async-done(((bf16[128,2048]{1,0:T(8,128)(2,1)}), bf16[2048,2048]{1,0:T(8,128)(2,1)}) %all-gather.11.cloned.1.call-update) | async-done | bytes 8388624 | tf_op jit(solution)/shard_map/all_gather | solution.py:59
  669.3 10.6 multiply_convert_fusion.1
  681.9 11.8 convolution_convert_fusion.1
  693.8 102.1 %reduce-scatter.12.cloned.1.call-done = bf16[128,2048]{1,0:T(8,128)(2,1)} async-done(((bf16[2048,2048]{1,0:T(8,128)(2,1)}), bf16[128,2048]{1,0:T(8,128)(2,1)}) %reduce-scatter.12.cloned.1.call-update) | async-done | bytes 524304 | tf_op jit(solution)/shard_map/reduce_scatter | solution.py:63
  800.5 12.6 %fusion.9 = f32[2048,1024]{1,0:T(8,128)S(1)} fusion(bf16[2048,2048]{1,0:T(8,128)(2,1)} %all-gather.9.cloned.1.call-done, bf16[2048,512]{0,1:T(8,128)(2,1)} %copy-done.35, bf16[2048,512]{0,1:T(8,128)(2,1)} %copy-done.34), kind=kOutput, calls=%fused_computation.23 | convolution fusion | flops 8598323200 | bytes 20971520 | tf_op jit(solution)/shard_map/dot_general | solution.py:45
  813.1 3.4 copy-done.16
  821.1 53.2 %all-gather.13.cloned.1.call-done = bf16[2048,2048]{1,0:T(8,128)(2,1)} async-done(((bf16[128,2048]{1,0:T(8,128)(2,1)}), bf16[2048,2048]{1,0:T(8,128)(2,1)}) %all-gather.13.cloned.1.call-update) | async-done | bytes 8388624 | tf_op jit(solution)/shard_map/all_gather | solution.py:59
  874.3 5.8 convolution_convert_fusion.4
  892.3 3.9 fusion.68
  899.3 60.0 %psum.22 = f32[2,2048]{1,0:T(2,128)S(1)} all-reduce(f32[2,2048]{1,0:T(2,128)S(1)} %pad_maximum_fusion.11), channel_id=1, replica_groups=mesh['rep'=2,'shard'=16] {'shard'}, use_global_device_ids=true, to_apply=%region_16.17 | all-reduce | flops 4096 | bytes 32768 | tf_op jit(solution)/shard_map/psum | solution.py:216
  959.4 3.1 multiply_convert_fusion.4
  963.0 9.8 convolution_convert_fusion
  972.8 5.0 fusion.5
  977.8 4.9 all-to-all-start.3
  982.8 7.3 fusion.95
  991.7 24.1 %collective-permute-done.6 = bf16[256,2048]{1,0:T(8,128)(2,1)S(1)} collective-permute-done((bf16[256,2048]{1,0:T(8,128)(2,1)S(1)}, bf16[256,2048]{1,0:T(8,128)(2,1)S(1)}, u32[]{:S(2)}, u32[]{:S(2)}) %collective-permute-start.6) | collective-permute-done | bytes 1048608 | tf_op jit(solution)/shard_map/ppermute | solution.py:75
  1018.5 20.4 %all-to-all-done.3 = bf16[16,64,1024]{2,1,0:T(8,128)(2,1)} async-done(((bf16[16,64,1024]{2,1,0:T(8,128)(2,1)}), bf16[16,64,1024]{2,1,0:T(8,128)(2,1)}, u32[]{:S(2)}, u32[]{:S(2)}) %all-to-all-start.3) | async-done | bytes 2097184 | tf_op jit(solution)/shard_map/all_to_all | solution.py:99
  1043.8 8.6 convolution_bitcast_fusion
  1057.2 4.2 bitcast_convert_fusion
  1061.4 22.4 %collective-permute-done.5 = bf16[16,64,1024]{2,1,0:T(8,128)(2,1)} collective-permute-done((bf16[16,64,1024]{2,1,0:T(8,128)(2,1)}, bf16[16,64,1024]{2,1,0:T(8,128)(2,1)}, u32[]{:S(2)}, u32[]{:S(2)}) %collective-permute-start.5) | collective-permute-done | bytes 2097184 | tf_op jit(solution)/shard_map/ppermute | solution.py:82
  1083.8 4.5 broadcast_select_fusion.1
  1088.3 4.5 stack.97
  1092.8 5.2 copy.134
  1098.0 4.7 stack.98
  1102.7 5.2 copy.135
  1110.0 32.8 %all-to-all-start.2 = ((bf16[16,64,384]{2,1,0:T(8,128)(2,1)}), bf16[16,64,384]{2,1,0:T(8,128)(2,1)}, u32[]{:S(2)}, u32[]{:S(2)}) async-start(bf16[16,64,384]{2,1,0:T(8,128)(2,1)} %fusion.15), calls=%async_computation.6 | async-start | bytes 1572864 | tf_op jit(solution)/shard_map/all_to_all | solution.py:99
  1142.9 4.9 fusion
  1149.2 3.8 convert_bitcast_fusion
  1153.1 9.4 reshape.428
  1165.2 7.6 psum.23
  1175.3 16.9 %collective-permute-done.1 = bf16[16,64,384]{2,1,0:T(8,128)(2,1)S(1)} collective-permute-done((bf16[16,64,384]{2,1,0:T(8,128)(2,1)}, bf16[16,64,384]{2,1,0:T(8,128)(2,1)S(1)}, u32[]{:S(2)}, u32[]{:S(2)}) %collective-permute-start.1) | collective-permute-done | bytes 786464 | tf_op jit(solution)/shard_map/ppermute | solution.py:82
  1195.4 3.5 copy.132
  1198.9 4.3 reshape.426
  (188 shorter events, 92.1 us)
Async XLA Ops:
  7.2 472.2 %copy-start = (bf16[512,2048]{1,0:T(8,128)(2,1)S(1)}, bf16[512,2048]{1,0:T(8,128)(2,1)}, u32[]{:S(2)}) copy-start(bf16[512,2048]{1,0:T(8,128)(2,1)} %param.17) | copy-start | bytes 6291460
  7.2 106.3 %all-gather.7.cloned.1.call-start = ((), (), s32[]{:S(2)}) async-start(), calls=%async_computation.9 | async-start | bytes 8912896 | tf_op jit(solution)/shard_map/all_gather | solution.py:59
  7.9 12.9 %copy-start.31 = (bf16[128]{0:T(256)(128)(2,1)S(1)}, bf16[128]{0:T(256)(128)(2,1)}, u32[]{:S(2)}) copy-start(bf16[128]{0:T(256)(128)(2,1)} %param.18) | copy-start | bytes 772
  7.9 12.9 %copy-start.32 = (bf16[128]{0:T(256)(128)(2,1)S(1)}, bf16[128]{0:T(256)(128)(2,1)}, u32[]{:S(2)}) copy-start(bf16[128]{0:T(256)(128)(2,1)} %param.19) | copy-start | bytes 772
  8.0 12.9 %copy-start.33 = (s32[128]{0:T(128)S(1)}, s32[128]{0:T(128)}, u32[]{:S(2)}) copy-start(s32[128]{0:T(128)} %param.12) | copy-start | bytes 1540
  8.0 12.9 %copy-start.29 = (bf16[128]{0:T(256)(128)(2,1)S(1)}, bf16[128]{0:T(256)(128)(2,1)}, u32[]{:S(2)}) copy-start(bf16[128]{0:T(256)(128)(2,1)} %param.21) | copy-start | bytes 772
  8.0 12.9 %copy-start.30 = (bf16[128]{0:T(256)(128)(2,1)S(1)}, bf16[128]{0:T(256)(128)(2,1)}, u32[]{:S(2)}) copy-start(bf16[128]{0:T(256)(128)(2,1)} %param.20) | copy-start | bytes 772
  13.3 66.8 %all-to-all-start = ((bf16[128,3,16,128]{0,3,1,2:T(8,128)(2,1)}), bf16[128,3,16,128]{0,3,1,2:T(8,128)(2,1)}, u32[]{:S(2)}, u32[]{:S(2)}) async-start(bf16[128,3,16,128]{0,3,1,2:T(8,128)(2,1)} %copy.114), calls=%async_computation | async-start | bytes 3145728 | tf_op jit(solution)/shard_map/all_to_all | solution.py:107
  20.8 282.0 %reduce-scatter.8.cloned.1.call-start = ((), (), s32[]{:S(2)}) async-start(), calls=%async_computation.10 | async-start | bytes 8912896 | tf_op jit(solution)/shard_map/reduce_scatter | solution.py:63
  201.8 260.3 %all-gather.9.cloned.1.call-start = ((), (), s32[]{:S(2)}) async-start(), calls=%async_computation.11 | async-start | bytes 8912896 | tf_op jit(solution)/shard_map/all_gather | solution.py:59
  306.3 283.5 %reduce-scatter.10.cloned.1.call-start = ((), (), s32[]{:S(2)}) async-start(), calls=%async_computation.12 | async-start | bytes 8912896 | tf_op jit(solution)/shard_map/reduce_scatter | solution.py:63
  474.7 3.4 copy-start.5
  486.3 183.0 %all-gather.11.cloned.1.call-start = ((), (), s32[]{:S(2)}) async-start(), calls=%async_computation.13 | async-start | bytes 8912896 | tf_op jit(solution)/shard_map/all_gather | solution.py:59
  595.2 200.7 %reduce-scatter.12.cloned.1.call-start = ((), (), s32[]{:S(2)}) async-start(), calls=%async_computation.14 | async-start | bytes 8912896 | tf_op jit(solution)/shard_map/reduce_scatter | solution.py:63
  669.3 12.6 %copy-start.20 = (bf16[16,128,2,1,512]{1,0,4,2,3:T(8,128)(2,1)S(1)}, bf16[16,128,2,1,512]{1,0,4,2,3:T(8,128)(2,1)}, u32[]{:S(2)}) copy-start(bf16[16,128,2,1,512]{1,0,4,2,3:T(8,128)(2,1)} %copy.122) | copy-start | bytes 12582916
  679.9 2.0 copy-start.35
  693.7 102.2 %copy-start.3 = (bf16[128,2048]{1,0:T(8,128)(2,1)S(1)}, bf16[128,2048]{1,0:T(8,128)(2,1)}, u32[]{:S(2)}) copy-start(bf16[128,2048]{1,0:T(8,128)(2,1)} %param.13) | copy-start | bytes 1572868
  693.7 102.2 %copy-start.6 = (bf16[128,2048]{1,0:T(8,128)(2,1)S(1)}, bf16[128,2048]{1,0:T(8,128)(2,1)}, u32[]{:S(2)}) copy-start(bf16[128,2048]{1,0:T(8,128)(2,1)} %reduce-scatter.8.cloned.1.call-done) | copy-start | bytes 1572868
  693.7 103.8 %copy-start.7 = (bf16[128,2048]{1,0:T(8,128)(2,1)S(1)}, bf16[128,2048]{1,0:T(8,128)(2,1)}, u32[]{:S(2)}) copy-start(bf16[128,2048]{1,0:T(8,128)(2,1)} %reduce-scatter.10.cloned.1.call-done) | copy-start | bytes 1572868
  693.7 103.8 %copy-start.12 = (bf16[128,2048]{1,0:T(8,128)(2,1)S(1)}, bf16[128,2048]{1,0:T(8,128)(2,1)}, u32[]{:S(2)}) copy-start(bf16[128,2048]{1,0:T(8,128)(2,1)} %param.11) | copy-start | bytes 1572868
  693.7 180.6 %all-gather.13.cloned.1.call-start = ((), (), s32[]{:S(2)}) async-start(), calls=%async_computation.15 | async-start | bytes 8912896 | tf_op jit(solution)/shard_map/all_gather | solution.py:59
  800.2 362.2 %reduce-scatter.16.cloned.1.call-start = ((), (), s32[]{:S(2)}) async-start(), calls=%async_computation.17 | async-start | bytes 1114112
  813.1 3.4 copy-start.16
  818.1 154.7 %collective-permute-start.4 = (bf16[16,64,1024]{2,1,0:T(8,128)(2,1)}, bf16[16,64,1024]{2,1,0:T(8,128)(2,1)}, u32[]{:S(2)}, u32[]{:S(2)}) collective-permute-start(bf16[16,64,1024]{2,1,0:T(8,128)(2,1)} %fusion.10), channel_id=1, source_target_pairs={{0,16},{16,0},{1,17},{17,1},{2,18},{18,2},{3,19},{19,3},{4,20},{20... | collective-permute-start | bytes 6291464 | tf_op jit(solution)/shard_map/ppermute | solution.py:75
  821.1 59.1 %copy-start.19 = (f32[16,128,1,128]{3,1,0,2:T(8,128)S(1)}, f32[16,128,1,128]{3,1,0,2:T(8,128)}, u32[]{:S(2)}) copy-start(f32[16,128,1,128]{3,1,0,2:T(8,128)} %get-tuple-element.68) | copy-start | bytes 3145732
  821.1 59.4 %copy-start.17 = (bf16[2048,128]{1,0:T(8,128)(2,1)S(1)}, bf16[2048,128]{1,0:T(8,128)(2,1)}, u32[]{:S(2)}) copy-start(bf16[2048,128]{1,0:T(8,128)(2,1)} %copy.144) | copy-start | bytes 1572868
  821.1 382.1 %reduce-scatter.14.cloned.1.call-start = ((), (), s32[]{:S(2)}) async-start(), calls=%async_computation.16 | async-start | bytes 8912896 | tf_op jit(solution)/shard_map/reduce_scatter | solution.py:63
  897.0 65.4 %copy-start.15 = (bf16[2048,128]{1,0:T(8,128)(2,1)S(1)}, bf16[2048,128]{1,0:T(8,128)(2,1)}, u32[]{:S(2)}) copy-start(bf16[2048,128]{1,0:T(8,128)(2,1)} %copy-done.14) | copy-start | bytes 1572868
  963.0 9.8 copy-start.27
  977.8 4.9 copy-start.22
  977.8 61.1 %all-to-all-start.3 = ((bf16[16,64,1024]{2,1,0:T(8,128)(2,1)}), bf16[16,64,1024]{2,1,0:T(8,128)(2,1)}, u32[]{:S(2)}, u32[]{:S(2)}) async-start(bf16[16,64,1024]{2,1,0:T(8,128)(2,1)} %fusion.5), calls=%async_computation.7 | async-start | bytes 4194304 | tf_op jit(solution)/shard_map/all_to_all | solution.py:99
  990.1 27.4 %copy-start.11 = (bf16[16,128,1,128]{3,1,0,2:T(8,128)(2,1)S(1)}, bf16[16,128,1,128]{3,1,0,2:T(8,128)(2,1)}, u32[]{:S(2)}) copy-start(bf16[16,128,1,128]{3,1,0,2:T(8,128)(2,1)} %copy-done.10) | copy-start | bytes 1572868
  990.2 25.5 %collective-permute-start.6 = (bf16[256,2048]{1,0:T(8,128)(2,1)S(1)}, bf16[256,2048]{1,0:T(8,128)(2,1)S(1)}, u32[]{:S(2)}, u32[]{:S(2)}) collective-permute-start(bf16[256,2048]{1,0:T(8,128)(2,1)S(1)} %fusion.45), channel_id=1, source_target_pairs={{0,16},{16,0},{1,17},{17,1},{2,18},{18,2},{3,19},{19,3},{4,20},{20... | collective-permute-start | bytes 3145736 | tf_op jit(solution)/shard_map/ppermute | solution.py:75
  1016.0 24.9 %collective-permute-start.7 = (bf16[256,2048]{1,0:T(8,128)(2,1)S(1)}, bf16[256,2048]{1,0:T(8,128)(2,1)}, u32[]{:S(2)}, u32[]{:S(2)}) collective-permute-start(bf16[256,2048]{1,0:T(8,128)(2,1)S(1)} %fusion.11), channel_id=1, source_target_pairs={{0,16},{16,0},{1,17},{17,1},{2,18},{18,2},{3,19},{19,3},{4,20},{20... | collective-permute-start | bytes 3145736 | tf_op jit(solution)/shard_map/ppermute | solution.py:82
  1018.5 25.3 %copy-start.25 = (bf16[2048,128]{0,1:T(8,128)(2,1)S(1)}, bf16[2048,128]{0,1:T(8,128)(2,1)}, u32[]{:S(2)}) copy-start(bf16[2048,128]{0,1:T(8,128)(2,1)} %get-tuple-element.26) | copy-start | bytes 1572868
  1018.5 25.3 %copy-start.26 = (bf16[2048,128]{0,1:T(8,128)(2,1)S(1)}, bf16[2048,128]{0,1:T(8,128)(2,1)}, u32[]{:S(2)}) copy-start(bf16[2048,128]{0,1:T(8,128)(2,1)} %get-tuple-element.27) | copy-start | bytes 1572868
  1038.9 4.8 copy-start.28
  1039.0 44.9 %collective-permute-start.5 = (bf16[16,64,1024]{2,1,0:T(8,128)(2,1)}, bf16[16,64,1024]{2,1,0:T(8,128)(2,1)}, u32[]{:S(2)}, u32[]{:S(2)}) collective-permute-start(bf16[16,64,1024]{2,1,0:T(8,128)(2,1)} %all-to-all-done.3), channel_id=1, source_target_pairs={{0,16},{16,0},{1,17},{17,1},{2,18},{18,2},{3,19},{19,3},{4,20},{20... | collective-permute-start | bytes 6291464 | tf_op jit(solution)/shard_map/ppermute | solution.py:82
  1055.8 52.1 %collective-permute-start = (bf16[16,64,384]{2,1,0:T(8,128)(2,1)}, bf16[16,64,384]{2,1,0:T(8,128)(2,1)}, u32[]{:S(2)}, u32[]{:S(2)}) collective-permute-start(bf16[16,64,384]{2,1,0:T(8,128)(2,1)} %fusion.50), channel_id=1, source_target_pairs={{0,16},{16,0},{1,17},{17,1},{2,18},{18,2},{3,19},{19,3},{4,20},{20... | collective-permute-start | bytes 2359304 | tf_op jit(solution)/shard_map/ppermute | solution.py:75
  1110.0 63.3 %all-to-all-start.2 = ((bf16[16,64,384]{2,1,0:T(8,128)(2,1)}), bf16[16,64,384]{2,1,0:T(8,128)(2,1)}, u32[]{:S(2)}, u32[]{:S(2)}) async-start(bf16[16,64,384]{2,1,0:T(8,128)(2,1)} %fusion.15), calls=%async_computation.6 | async-start | bytes 1572864 | tf_op jit(solution)/shard_map/all_to_all | solution.py:99
  1142.9 6.4 copy-start.8
  1142.9 6.4 copy-start.9
  1147.9 15.4 %collective-permute-start.2 = (bf16[64,2048]{1,0:T(8,128)(2,1)S(1)}, bf16[64,2048]{1,0:T(8,128)(2,1)}, u32[]{:S(2)}, u32[]{:S(2)}) collective-permute-start(bf16[64,2048]{1,0:T(8,128)(2,1)S(1)} %fusion.81), channel_id=1, source_target_pairs={{0,16},{16,0},{1,17},{17,1},{2,18},{18,2},{3,19},{19,3},{4,20},{20... | collective-permute-start | bytes 786440 | tf_op jit(solution)/shard_map/ppermute | solution.py:75
  1164.4 9.7 collective-permute-start.3
  1173.3 18.9 %collective-permute-start.1 = (bf16[16,64,384]{2,1,0:T(8,128)(2,1)}, bf16[16,64,384]{2,1,0:T(8,128)(2,1)S(1)}, u32[]{:S(2)}, u32[]{:S(2)}) collective-permute-start(bf16[16,64,384]{2,1,0:T(8,128)(2,1)} %all-to-all-done.2), channel_id=1, source_target_pairs={{0,16},{16,0},{1,17},{17,1},{2,18},{18,2},{3,19},{19,3},{4,20},{20... | collective-permute-start | bytes 2359304 | tf_op jit(solution)/shard_map/ppermute | solution.py:82
  1195.4 10.2 copy-start.1
  1198.9 4.3 copy-start.4
  1198.9 4.3 copy-start.13
  (8 other events, 9.5 us)
Sparse Core Ops, SparseCore 0:
  10.2 103.3 all-gather.6
  202.0 100.8 reduce-scatter.7
  306.4 134.0 all-gather.8
  486.4 103.4 reduce-scatter.9
  595.3 73.9 all-gather.10
  693.8 102.0 reduce-scatter.11
  800.3 73.9 all-gather.12
  877.9 56.2 reduce-scatter.15
  972.9 130.3 reduce-scatter.13
where the time goes:
time: 1220 us; the launch traced here: 1210 us
  waiting for transfers between devices  549 us (45%)
  blocking collectives  327 us (27%)
  matrix products  110 us (9%)
  local copies, waits for them, and re-layouts  96.8 us (8%)
  other arithmetic  59.2 us (5%)
  starting transfers between devices  56 us (5%)
  between operations  14.8 us (1%)
    reduce_scatter x4, waiting for transfers between devices, scatter(): lax.psum_scatter(partial.astype(BF), 'shard', scatter_dimension=0, tiled=...  307 us
    all_gather x4, waiting for transfers between devices, gather(): return lax.all_gather(piece, 'shard', axis=0, tiled=True)  157 us
    all_to_all x1, blocking collectives, columns(): w = lax.all_to_all(w, 'shard', split_axis=2, concat_axis=0, tiled=True)  142 us
    psum x1, blocking collectives, shards(): inner = lax.psum(inner, 'shard') / width  60 us
    psum x1, blocking collectives, shards(): squares = lax.psum(squares, 'shard')  58.7 us
    all_gather x1, blocking collectives, gather(): return lax.all_gather(piece, 'shard', axis=0, tiled=True)  58.7 us
    ppermute x4, waiting for transfers between devices, rep_gather(): got = lax.ppermute(x, 'rep', [(0, 1), (1, 0)])  40 us
    dot_general x4, matrix products, mm_nt(): lax.dot_general(left, right, (((1,), (1,)), ((), ())), preferred_element_...  37.9 us
  transfers between devices with their start and end apart: 20, of which 11 were waited for; matrix products, arithmetic and copies ran while one was open for 14% of the time, Pallas kernels for 0%

commit v1 on v0

--- a/solution.py
+++ b/solution.py
@@ -8,6 +8,11 @@
 THETA = 500000.0
 BF = jnp.bfloat16
 F32 = jnp.float32
+
+
+def exchange_gather(block, mesh_axis, d):
+    sent = jnp.stack([block] * lax.axis_size(mesh_axis))
+    return jnp.concatenate(lax.all_to_all(sent, mesh_axis, 0, 0), axis=d)
 
 
 def positions(seg):
@@ -56,7 +61,7 @@
 
 
 def gather(piece):
-    return lax.all_gather(piece, "shard", axis=0, tiled=True)
+    return exchange_gather(piece, "shard", 0)
 
 
 def scatter(partial):

time: 1220 us -> 1730 us (1.42)
  waiting for transfers between devices: 549 us -> 886 us
  blocking collectives: 327 us -> 421 us
  local copies, waits for them, and re-layouts: 96.8 us -> 150 us
  starting transfers between devices: 56 us -> 75.5 us
    all_to_all x0 -> x4, waiting for transfers between devices: none -> 415 us  [exchange_gather(): return jnp.concatenate(lax.all_to_all(sent, mesh_axis, 0, 0), axis=d)]
    all_to_all x0 -> x1, blocking collectives: none -> 186 us  [exchange_gather(): return jnp.concatenate(lax.all_to_all(sent, mesh_axis, 0, 0), axis=d)]
    all_gather x4 -> x0, waiting for transfers between devices: 157 us -> none  [gather(): return lax.all_gather(piece, 'shard', axis=0, tiled=True)]
    all_to_all x1, blocking collectives: 142 us -> 40.9 us  [columns(): w = lax.all_to_all(w, 'shard', split_axis=2, concat_axis=0, tiled=True)]
    reduce_scatter x4, waiting for transfers between devices: 307 us -> 385 us  [scatter(): lax.psum_scatter(partial.astype(BF), 'shard', scatter_dimension=0, tiled=...]
    all_gather x1 -> x0, blocking collectives: 58.7 us -> none  [gather(): return lax.all_gather(piece, 'shard', axis=0, tiled=True)]
    psum x1, blocking collectives: 58.7 us -> 92.7 us  [shards(): squares = lax.psum(squares, 'shard')]
    psum x1, blocking collectives: 60 us -> 92.8 us  [shards(): inner = lax.psum(inner, 'shard') / width]
  transfers between devices with their start and end apart: 20 -> 20, of which waited for: 11 -> 12; matrix products, arithmetic and copies ran while one was open for 14% -> 11% of each run, Pallas kernels for 0% -> 0%
where the time goes in v1:
time: 1730 us; the launch traced here: 1720 us
  waiting for transfers between devices  886 us (51%)
  blocking collectives  421 us (24%)
  local copies, waits for them, and re-layouts  150 us (9%)
  matrix products  108 us (6%)
  starting transfers between devices  75.5 us (4%)
  other arithmetic  61.7 us (4%)
    all_to_all x4, waiting for transfers between devices, exchange_gather(): return jnp.concatenate(lax.all_to_all(sent, mesh_axis, 0, 0), axis=d)  415 us
    reduce_scatter x4, waiting for transfers between devices, scatter(): lax.psum_scatter(partial.astype(BF), 'shard', scatter_dimension=0, tiled=...  385 us
    all_to_all x1, blocking collectives, exchange_gather(): return jnp.concatenate(lax.all_to_all(sent, mesh_axis, 0, 0), axis=d)  186 us
    psum x1, blocking collectives, shards(): inner = lax.psum(inner, 'shard') / width  92.8 us
    psum x1, blocking collectives, shards(): squares = lax.psum(squares, 'shard')  92.7 us
    ppermute x4, waiting for transfers between devices, rep_gather(): got = lax.ppermute(x, 'rep', [(0, 1), (1, 0)])  41.9 us
    all_to_all x1, blocking collectives, columns(): w = lax.all_to_all(w, 'shard', split_axis=2, concat_axis=0, tiled=True)  40.9 us
    all_to_all x2, starting transfers between devices, grad_back(): lax.all_to_all(part, 'shard', split_axis=0, concat_axis=0, tiled=True)  37.5 us
  transfers between devices with their start and end apart: 20, of which 12 were waited for; matrix products, arithmetic and copies ran while one was open for 11% of the time, Pallas kernels for 0%

profile of v1, /device:TPU:0, one launch (start us, length us, event | category | flops | bytes accessed | tf_op | source)
XLA Modules:
  0.0 1717.4 jit_solution(5755267799322481953)
XLA Ops:
  9.3 7.4 all-to-all-start.2
  23.2 40.9 %all_to_all.65 = bf16[128,3,16,128]{0,3,1,2:T(8,128)(2,1)} all-to-all(bf16[128,3,16,128]{0,3,1,2:T(8,128)(2,1)} %copy.119), channel_id=1, replica_groups=mesh['rep'=2,'shard'=16] {'shard'}, dimensions={2} | all-to-all | bytes 3145728 | tf_op jit(solution)/shard_map/all_to_all | solution.py:112
  64.1 4.5 stack.64
  68.6 5.2 all-to-all-start
  78.1 146.4 %all-to-all-done = bf16[16,128,2048]{2,1,0:T(8,128)(2,1)} async-done(((bf16[16,128,2048]{2,1,0:T(8,128)(2,1)}), bf16[16,128,2048]{2,1,0:T(8,128)(2,1)}, u32[]{:S(2)}, u32[]{:S(2)}) %all-to-all-start) | async-done | bytes 8388640 | tf_op jit(solution)/shard_map/all_to_all | solution.py:15
  224.4 6.4 fusion.12
  233.4 92.7 %psum.21 = f32[2,2048]{1,0:T(2,128)S(1)} all-reduce(f32[2,2048]{1,0:T(2,128)S(1)} %pad_maximum_fusion.10), channel_id=1, replica_groups=mesh['rep'=2,'shard'=16] {'shard'}, use_global_device_ids=true, to_apply=%region_2.3 | all-reduce | flops 4096 | bytes 32768 | tf_op jit(solution)/shard_map/psum | solution.py:149
  340.1 6.8 convolution_convert_fusion.3
  346.9 6.5 copy.127
  353.3 5.1 copy.128
  358.4 4.7 all-to-all-start.4
  363.2 145.7 %reduce-scatter.8.cloned.1.call-done = bf16[128,2048]{1,0:T(8,128)(2,1)} async-done(((bf16[2048,2048]{1,0:T(8,128)(2,1)}), bf16[128,2048]{1,0:T(8,128)(2,1)}) %reduce-scatter.8.cloned.1.call-update) | async-done | bytes 524304 | tf_op jit(solution)/shard_map/reduce_scatter | solution.py:68
  514.4 6.1 stack.73
  520.4 4.8 all-to-all-start.3
  525.3 6.9 copy.129
  532.2 143.6 %all-to-all-done.3 = bf16[16,128,2048]{1,2,0:T(8,128)(2,1)} async-done(((bf16[16,128,2048]{1,2,0:T(8,128)(2,1)}), bf16[16,128,2048]{1,2,0:T(8,128)(2,1)}, u32[]{:S(2)}, u32[]{:S(2)}) %all-to-all-start.3) | async-done | bytes 8388640 | tf_op jit(solution)/shard_map/all_to_all | solution.py:15
  675.7 12.2 copy.126
  688.0 12.5 fusion.1
  705.1 6.9 convolution_convert_fusion.2
  712.7 134.8 %reduce-scatter.10.cloned.1.call-done = bf16[128,2048]{1,0:T(8,128)(2,1)} async-done(((bf16[2048,2048]{1,0:T(8,128)(2,1)}), bf16[128,2048]{1,0:T(8,128)(2,1)}) %reduce-scatter.10.cloned.1.call-update) | async-done | bytes 524304 | tf_op jit(solution)/shard_map/reduce_scatter | solution.py:68
  853.0 186.5 %all_to_all.66 = bf16[16,128,2048]{2,1,0:T(8,128)(2,1)} all-to-all(bf16[16,128,2048]{2,1,0:T(8,128)(2,1)S(1)} %stack.74), channel_id=1, replica_groups=mesh['rep'=2,'shard'=16] {'shard'}, dimensions={0} | all-to-all | bytes 16777216 | tf_op jit(solution)/shard_map/all_to_all | solution.py:15
  1039.5 9.6 multiply_convert_fusion.1
  1051.2 11.8 convolution_convert_fusion.1
  1063.0 104.7 %reduce-scatter.12.cloned.1.call-done = bf16[128,2048]{1,0:T(8,128)(2,1)} async-done(((bf16[2048,2048]{1,0:T(8,128)(2,1)}), bf16[128,2048]{1,0:T(8,128)(2,1)}) %reduce-scatter.12.cloned.1.call-update) | async-done | bytes 524304 | tf_op jit(solution)/shard_map/reduce_scatter | solution.py:68
  1176.1 4.8 all-to-all-start.6
  1181.4 12.5 copy.141
  1193.9 12.0 fusion.4
  1213.8 124.0 %all-to-all-done.6 = bf16[16,128,2048]{2,1,0:T(8,128)(2,1)} async-done(((bf16[16,128,2048]{2,1,0:T(8,128)(2,1)}), bf16[16,128,2048]{2,1,0:T(8,128)(2,1)}, u32[]{:S(2)}, u32[]{:S(2)}) %all-to-all-start.6) | async-done | bytes 8388640 | tf_op jit(solution)/shard_map/all_to_all | solution.py:15
  1337.8 5.9 convolution_convert_fusion.4
  1363.8 92.8 %psum.22 = f32[2,2048]{1,0:T(2,128)S(1)} all-reduce(f32[2,2048]{1,0:T(2,128)S(1)} %pad_maximum_fusion.11), channel_id=1, replica_groups=mesh['rep'=2,'shard'=16] {'shard'}, use_global_device_ids=true, to_apply=%region_16.17 | all-reduce | flops 4096 | bytes 32768 | tf_op jit(solution)/shard_map/psum | solution.py:221
  1462.3 8.2 convolution_convert_fusion
  1470.5 5.0 fusion.3
  1475.5 4.8 all-to-all-start.8
  1480.3 7.3 fusion.95
  1489.2 23.9 %collective-permute-done.6 = bf16[256,2048]{1,0:T(8,128)(2,1)S(1)} collective-permute-done((bf16[256,2048]{1,0:T(8,128)(2,1)S(1)}, bf16[256,2048]{1,0:T(8,128)(2,1)S(1)}, u32[]{:S(2)}, u32[]{:S(2)}) %collective-permute-start.6) | collective-permute-done | bytes 1048608 | tf_op jit(solution)/shard_map/ppermute | solution.py:80
  1515.9 20.5 %all-to-all-done.8 = bf16[16,64,1024]{2,1,0:T(8,128)(2,1)} async-done(((bf16[16,64,1024]{2,1,0:T(8,128)(2,1)}), bf16[16,64,1024]{2,1,0:T(8,128)(2,1)}, u32[]{:S(2)}, u32[]{:S(2)}) %all-to-all-start.8) | async-done | bytes 2097184 | tf_op jit(solution)/shard_map/all_to_all | solution.py:104
  1541.1 8.6 convolution_bitcast_fusion
  1557.0 24.3 %collective-permute-done.5 = bf16[16,64,1024]{2,1,0:T(8,128)(2,1)} collective-permute-done((bf16[16,64,1024]{2,1,0:T(8,128)(2,1)}, bf16[16,64,1024]{2,1,0:T(8,128)(2,1)}, u32[]{:S(2)}, u32[]{:S(2)}) %collective-permute-start.5) | collective-permute-done | bytes 2097184 | tf_op jit(solution)/shard_map/ppermute | solution.py:87
  1581.3 4.5 broadcast_select_fusion.1
  1589.2 4.5 stack.86
  1593.7 5.0 fusion.94
  1602.4 32.8 %all-to-all-start.7 = ((bf16[16,64,384]{2,1,0:T(8,128)(2,1)}), bf16[16,64,384]{2,1,0:T(8,128)(2,1)}, u32[]{:S(2)}, u32[]{:S(2)}) async-start(bf16[16,64,384]{2,1,0:T(8,128)(2,1)} %fusion.14), calls=%async_computation.11 | async-start | bytes 1572864 | tf_op jit(solution)/shard_map/all_to_all | solution.py:104
  1635.2 10.4 convert_bitcast_fusion
  1645.6 11.5 copy.143
  1657.1 9.4 reshape.454
  1669.2 8.0 psum.23
  1679.8 17.3 %collective-permute-done.1 = bf16[16,64,384]{2,1,0:T(8,128)(2,1)S(1)} collective-permute-done((bf16[16,64,384]{2,1,0:T(8,128)(2,1)}, bf16[16,64,384]{2,1,0:T(8,128)(2,1)S(1)}, u32[]{:S(2)}, u32[]{:S(2)}) %collective-permute-start.1) | collective-permute-done | bytes 786464 | tf_op jit(solution)/shard_map/ppermute | solution.py:87
  1703.7 4.3 reshape.452
  (222 shorter events, 127.7 us)
Async XLA Ops:
  7.2 698.0 %copy-start = (bf16[512,2048]{1,0:T(8,128)(2,1)S(1)}, bf16[512,2048]{1,0:T(8,128)(2,1)}, u32[]{:S(2)}) copy-start(bf16[512,2048]{1,0:T(8,128)(2,1)} %param.17) | copy-start | bytes 6291460
  9.3 13.9 all-to-all-start.2
  16.7 47.4 %copy-start.11 = (bf16[128,2048]{1,0:T(8,128)(2,1)S(1)}, bf16[128,2048]{1,0:T(8,128)(2,1)}, u32[]{:S(2)}) copy-start(bf16[128,2048]{1,0:T(8,128)(2,1)} %param.11) | copy-start | bytes 1572868
  68.6 155.8 %all-to-all-start = ((bf16[16,128,2048]{2,1,0:T(8,128)(2,1)}), bf16[16,128,2048]{2,1,0:T(8,128)(2,1)}, u32[]{:S(2)}, u32[]{:S(2)}) async-start(bf16[16,128,2048]{2,1,0:T(8,128)(2,1)} %stack.64), calls=%async_computation | async-start | bytes 16777216 | tf_op jit(solution)/shard_map/all_to_all | solution.py:15
  73.9 434.9 %reduce-scatter.8.cloned.1.call-start = ((), (), s32[]{:S(2)}) async-start(), calls=%async_computation.14 | async-start | bytes 8912896 | tf_op jit(solution)/shard_map/reduce_scatter | solution.py:68
  74.0 252.2 %copy-start.37 = (f32[128]{0:T(128)}, f32[128]{0:T(128)S(1)}, u32[]{:S(2)}) copy-start(f32[128]{0:T(128)S(1)} %convert_element_type.225) | copy-start | bytes 1540
  74.0 252.2 %copy-start.39 = (f32[128]{0:T(128)}, f32[128]{0:T(128)S(1)}, u32[]{:S(2)}) copy-start(f32[128]{0:T(128)S(1)} %convert_element_type.229) | copy-start | bytes 1540
  74.0 254.0 %copy-start.41 = (f32[64]{0:T(128)}, f32[64]{0:T(128)S(1)}, u32[]{:S(2)}) copy-start(f32[64]{0:T(128)S(1)} %multiply_power_fusion) | copy-start | bytes 772
  74.5 253.5 %copy-start.35 = (f32[2048]{0:T(1024)}, f32[2048]{0:T(1024)S(1)}, u32[]{:S(2)}) copy-start(f32[2048]{0:T(1024)S(1)} %convert_bitcast_fusion.2) | copy-start | bytes 24580
  358.4 155.9 %all-to-all-start.4 = ((bf16[128,2,16,512]{0,3,1,2:T(8,128)(2,1)}), bf16[128,2,16,512]{0,3,1,2:T(8,128)(2,1)}, u32[]{:S(2)}, u32[]{:S(2)}) async-start(bf16[128,2,16,512]{0,3,1,2:T(8,128)(2,1)} %copy.128), calls=%async_computation.5 | async-start | bytes 8388608 | tf_op jit(solution)/shard_map/all_to_all | solution.py:112
  520.4 155.3 %all-to-all-start.3 = ((bf16[16,128,2048]{1,2,0:T(8,128)(2,1)}), bf16[16,128,2048]{1,2,0:T(8,128)(2,1)}, u32[]{:S(2)}, u32[]{:S(2)}) async-start(bf16[16,128,2048]{1,2,0:T(8,128)(2,1)} %stack.73), calls=%async_computation.4 | async-start | bytes 16777216 | tf_op jit(solution)/shard_map/all_to_all | solution.py:15
  525.2 322.3 %reduce-scatter.10.cloned.1.call-start = ((), (), s32[]{:S(2)}) async-start(), calls=%async_computation.15 | async-start | bytes 8912896 | tf_op jit(solution)/shard_map/reduce_scatter | solution.py:68
  712.1 455.6 %reduce-scatter.12.cloned.1.call-start = ((), (), s32[]{:S(2)}) async-start(), calls=%async_computation.16 | async-start | bytes 8912896 | tf_op jit(solution)/shard_map/reduce_scatter | solution.py:68
  852.0 187.6 %slice-start = ((s8[8388608]{0:T(1024)(128)(4,1)}), s8[4194304]{0:T(1024)(128)(4,1)S(1)}, s32[]{:S(2)}) async-start(s8[8388608]{0:T(1024)(128)(4,1)} %bitcast.206), calls=%async_computation.19 | async-start | bytes 8388608
  853.0 186.5 %slice-start.1 = ((s8[8388608]{0:T(1024)(128)(4,1)}), s8[4194304]{0:T(1024)(128)(4,1)S(1)}, s32[]{:S(2)}) async-start(s8[8388608]{0:T(1024)(128)(4,1)} %bitcast.206), calls=%async_computation.20 | async-start | bytes 8388608
  1039.5 11.6 copy-start.20
  1062.9 104.7 %copy-start.3 = (bf16[128,2048]{1,0:T(8,128)(2,1)S(1)}, bf16[128,2048]{1,0:T(8,128)(2,1)}, u32[]{:S(2)}) copy-start(bf16[128,2048]{1,0:T(8,128)(2,1)} %param.13) | copy-start | bytes 1572868
  1062.9 104.7 %copy-start.7 = (bf16[128,2048]{1,0:T(8,128)(2,1)S(1)}, bf16[128,2048]{1,0:T(8,128)(2,1)}, u32[]{:S(2)}) copy-start(bf16[128,2048]{1,0:T(8,128)(2,1)} %reduce-scatter.8.cloned.1.call-done) | copy-start | bytes 1572868
  1062.9 106.3 %copy-start.8 = (bf16[128,2048]{1,0:T(8,128)(2,1)S(1)}, bf16[128,2048]{1,0:T(8,128)(2,1)}, u32[]{:S(2)}) copy-start(bf16[128,2048]{1,0:T(8,128)(2,1)} %reduce-scatter.10.cloned.1.call-done) | copy-start | bytes 1572868
  1062.9 106.3 %copy-start.12 = (bf16[128,2048]{1,0:T(8,128)(2,1)S(1)}, bf16[128,2048]{1,0:T(8,128)(2,1)}, u32[]{:S(2)}) copy-start(bf16[128,2048]{1,0:T(8,128)(2,1)} %param.11) | copy-start | bytes 1572868
  1176.1 161.7 %all-to-all-start.6 = ((bf16[16,128,2048]{2,1,0:T(8,128)(2,1)}), bf16[16,128,2048]{2,1,0:T(8,128)(2,1)}, u32[]{:S(2)}, u32[]{:S(2)}) async-start(bf16[16,128,2048]{2,1,0:T(8,128)(2,1)} %stack.75), calls=%async_computation.9 | async-start | bytes 16777216 | tf_op jit(solution)/shard_map/all_to_all | solution.py:15
  1180.9 485.6 %reduce-scatter.16.cloned.1.call-start = ((), (), s32[]{:S(2)}) async-start(), calls=%async_computation.18 | async-start | bytes 1114112
  1181.4 12.5 copy-start.47
  1210.9 259.6 %collective-permute-start.4 = (bf16[16,64,1024]{2,1,0:T(8,128)(2,1)}, bf16[16,64,1024]{2,1,0:T(8,128)(2,1)}, u32[]{:S(2)}, u32[]{:S(2)}) collective-permute-start(bf16[16,64,1024]{2,1,0:T(8,128)(2,1)} %fusion.9), channel_id=1, source_target_pairs={{0,16},{16,0},{1,17},{17,1},{2,18},{18,2},{3,19},{19,3},{4,20},{20... | collective-permute-start | bytes 6291464 | tf_op jit(solution)/shard_map/ppermute | solution.py:80
  1213.8 494.3 %reduce-scatter.14.cloned.1.call-start = ((), (), s32[]{:S(2)}) async-start(), calls=%async_computation.17 | async-start | bytes 8912896 | tf_op jit(solution)/shard_map/reduce_scatter | solution.py:68
  1337.8 5.9 copy-start.19
  1337.8 6.3 copy-start.17
  1349.6 7.2 copy-start.36
  1349.6 7.2 copy-start.42
  1353.2 8.4 copy-start.32
  1353.2 8.4 copy-start.34
  1353.2 8.4 copy-start.38
  1353.2 8.4 copy-start.40
  1356.7 99.9 %copy-start.15 = (bf16[2048,128]{1,0:T(8,128)(2,1)S(1)}, bf16[2048,128]{1,0:T(8,128)(2,1)}, u32[]{:S(2)}) copy-start(bf16[2048,128]{1,0:T(8,128)(2,1)} %copy-done.14) | copy-start | bytes 1572868
  1459.0 11.4 copy-start.29
  1461.5 9.0 copy-start.25
  1475.5 60.9 %all-to-all-start.8 = ((bf16[16,64,1024]{2,1,0:T(8,128)(2,1)}), bf16[16,64,1024]{2,1,0:T(8,128)(2,1)}, u32[]{:S(2)}, u32[]{:S(2)}) async-start(bf16[16,64,1024]{2,1,0:T(8,128)(2,1)} %fusion.3), calls=%async_computation.12 | async-start | bytes 4194304 | tf_op jit(solution)/shard_map/all_to_all | solution.py:104
  1487.6 27.3 %copy-start.10 = (bf16[16,128,1,128]{3,1,0,2:T(8,128)(2,1)S(1)}, bf16[16,128,1,128]{3,1,0,2:T(8,128)(2,1)}, u32[]{:S(2)}) copy-start(bf16[16,128,1,128]{3,1,0,2:T(8,128)(2,1)} %copy-done.9) | copy-start | bytes 1572868
  1487.8 25.4 %collective-permute-start.6 = (bf16[256,2048]{1,0:T(8,128)(2,1)S(1)}, bf16[256,2048]{1,0:T(8,128)(2,1)S(1)}, u32[]{:S(2)}, u32[]{:S(2)}) collective-permute-start(bf16[256,2048]{1,0:T(8,128)(2,1)S(1)} %fusion.44), channel_id=1, source_target_pairs={{0,16},{16,0},{1,17},{17,1},{2,18},{18,2},{3,19},{19,3},{4,20},{20... | collective-permute-start | bytes 3145736 | tf_op jit(solution)/shard_map/ppermute | solution.py:80
  1513.4 24.6 %collective-permute-start.7 = (bf16[256,2048]{1,0:T(8,128)(2,1)S(1)}, bf16[256,2048]{1,0:T(8,128)(2,1)S(1)}, u32[]{:S(2)}, u32[]{:S(2)}) collective-permute-start(bf16[256,2048]{1,0:T(8,128)(2,1)S(1)} %fusion.10), channel_id=1, source_target_pairs={{0,16},{16,0},{1,17},{17,1},{2,18},{18,2},{3,19},{19,3},{4,20},{20... | collective-permute-start | bytes 3145736 | tf_op jit(solution)/shard_map/ppermute | solution.py:87
  1536.5 44.8 %collective-permute-start.5 = (bf16[16,64,1024]{2,1,0:T(8,128)(2,1)}, bf16[16,64,1024]{2,1,0:T(8,128)(2,1)}, u32[]{:S(2)}, u32[]{:S(2)}) collective-permute-start(bf16[16,64,1024]{2,1,0:T(8,128)(2,1)} %all-to-all-done.8), channel_id=1, source_target_pairs={{0,16},{16,0},{1,17},{17,1},{2,18},{18,2},{3,19},{19,3},{4,20},{20... | collective-permute-start | bytes 6291464 | tf_op jit(solution)/shard_map/ppermute | solution.py:87
  1555.6 44.5 %collective-permute-start = (bf16[16,64,384]{2,1,0:T(8,128)(2,1)}, bf16[16,64,384]{2,1,0:T(8,128)(2,1)}, u32[]{:S(2)}, u32[]{:S(2)}) collective-permute-start(bf16[16,64,384]{2,1,0:T(8,128)(2,1)} %fusion.49), channel_id=1, source_target_pairs={{0,16},{16,0},{1,17},{17,1},{2,18},{18,2},{3,19},{19,3},{4,20},{20... | collective-permute-start | bytes 2359304 | tf_op jit(solution)/shard_map/ppermute | solution.py:80
  1593.7 6.5 copy-start.5
  1598.7 68.6 %collective-permute-start.2 = (bf16[64,2048]{1,0:T(8,128)(2,1)S(1)}, bf16[64,2048]{1,0:T(8,128)(2,1)}, u32[]{:S(2)}, u32[]{:S(2)}) collective-permute-start(bf16[64,2048]{1,0:T(8,128)(2,1)S(1)} %fusion.80), channel_id=1, source_target_pairs={{0,16},{16,0},{1,17},{17,1},{2,18},{18,2},{3,19},{19,3},{4,20},{20... | collective-permute-start | bytes 786440 | tf_op jit(solution)/shard_map/ppermute | solution.py:80
  1602.4 75.3 %all-to-all-start.7 = ((bf16[16,64,384]{2,1,0:T(8,128)(2,1)}), bf16[16,64,384]{2,1,0:T(8,128)(2,1)}, u32[]{:S(2)}, u32[]{:S(2)}) async-start(bf16[16,64,384]{2,1,0:T(8,128)(2,1)} %fusion.14), calls=%async_computation.11 | async-start | bytes 1572864 | tf_op jit(solution)/shard_map/all_to_all | solution.py:104
  1668.4 10.2 collective-permute-start.3
  1677.8 19.3 %collective-permute-start.1 = (bf16[16,64,384]{2,1,0:T(8,128)(2,1)}, bf16[16,64,384]{2,1,0:T(8,128)(2,1)S(1)}, u32[]{:S(2)}, u32[]{:S(2)}) collective-permute-start(bf16[16,64,384]{2,1,0:T(8,128)(2,1)} %all-to-all-done.7), channel_id=1, source_target_pairs={{0,16},{16,0},{1,17},{17,1},{2,18},{18,2},{3,19},{19,3},{4,20},{20... | collective-permute-start | bytes 2359304 | tf_op jit(solution)/shard_map/ppermute | solution.py:87
  1700.3 10.1 copy-start.1
  (23 other events, 60.8 us)
Sparse Core Ops, SparseCore 0:
  347.0 161.7 reduce-scatter.7
  712.2 135.2 reduce-scatter.9
  1063.1 104.5 reduce-scatter.11
  1213.9 135.5 reduce-scatter.15
  1470.6 130.2 reduce-scatter.13
